TPU v7x, 32 devices: a whole 2x2x4 slice. The times are simulated.
32 devices in a mesh: rows: 4 (over y, x), tp: 8 (over z, core).
Axes of the slice: x: 2, y: 2, z: 4, core: 2. Of those that a mesh axis runs over, the one named last changes fastest.
Arguments:
- train_gate: float32 [3584, 14336], P('rows', 'tp'), may hold values from -0.125 to 0.125
- drift_gate: float32 [3584, 14336], P('rows', 'tp'), may hold values from -6 to 6
- spread_gate: float32 [3584, 14336], P('rows', 'tp'), may hold values from 0.1 to 10
- train_up: float32 [3584, 14336], P('rows', 'tp'), may hold values from -0.125 to 0.125
- drift_up: float32 [3584, 14336], P('rows', 'tp'), may hold values from -6 to 6
- spread_up: float32 [3584, 14336], P('rows', 'tp'), may hold values from 0.1 to 10
- norm_gain: float32 [3584], P('rows'), may hold values from 0.25 to 1.75
Outputs:
- serving_gate: bfloat16 [3584, 14336], P(None, 'tp')
- serving_up: bfloat16 [3584, 14336], P(None, 'tp')
- column_gate: float32 [14336], P('tp')
- column_up: float32 [14336], P('tp')
All inputs are finite; a program needn't handle non-finite values. Where the computation divides by a largest or mean magnitude, that divisor is 1e-20 or more.
Results may differ from a plain program's by a relative error of at most 0.001.
Values may be sent and summed in bfloat16 or wider, within the bound.
A program may use at most 128 MiB of HBM per device.

v0:
```python
import jax
import jax.numpy as jnp
from jax import lax
from jax.sharding import PartitionSpec as P

learn_rate = 0.015
decay_rate = 0.1
tiny_value = 1e-08


def per_device(train_gate, drift_gate, spread_gate, train_up, drift_up, spread_up, norm_gain):
    whole_gate = train_gate - learn_rate * (
        drift_gate / (jnp.sqrt(spread_gate) + tiny_value) + decay_rate * train_gate
    )
    whole_up = train_up - learn_rate * (
        drift_up / (jnp.sqrt(spread_up) + tiny_value) + decay_rate * train_up
    )
    whole_gained_gate = whole_gate * norm_gain[:, None]
    whole_gained_up = whole_up * norm_gain[:, None]
    column_gate, column_up = lax.pmax(
        (jnp.max(jnp.abs(whole_gained_gate), axis=0), jnp.max(jnp.abs(whole_gained_up), axis=0)),
        "rows",
    )
    narrow_gate, narrow_up = (
        (whole_gained_gate / column_gate).astype(jnp.bfloat16),
        (whole_gained_up / column_up).astype(jnp.bfloat16),
    )
    serving_gate, serving_up = (
        lax.all_gather(narrow_gate, "rows", axis=0, tiled=True),
        lax.all_gather(narrow_up, "rows", axis=0, tiled=True),
    )
    return (serving_gate, serving_up, column_gate, column_up)


def solution(mesh):
    return jax.shard_map(
        per_device,
        mesh=mesh,
        in_specs=(
            P("rows", "tp"),
            P("rows", "tp"),
            P("rows", "tp"),
            P("rows", "tp"),
            P("rows", "tp"),
            P("rows", "tp"),
            P("rows"),
        ),
        out_specs=(P(None, "tp"), P(None, "tp"), P("tp"), P("tp")),
        check_vma=False,
    )
```

profile of v0, /device:TPU:0, one launch (start us, length us, event | category | flops | bytes accessed | tf_op | source)
XLA Modules:
  0.0 326.3 jit_solution(2007188606949628659)
XLA Ops:
  7.2 0.0 all-gather.3.cloned.1.call-start
  7.2 20.6 %abs_reduce_fusion = (f32[1792]{0:T(1024)S(1)}, f32[896,1792]{1,0:T(8,128)}, f32[1792]{0:T(1024)S(1)}, f32[896,1792]{1,0:T(8,128)}) fusion(f32[896]{0:T(1024)} %param.13, f32[896,1792]{1,0:T(8,128)} %param.10, f32[896,1792]{1,0:T(8,128)} %param.11, f32[896,1792]{1,0:T(8,128)} %param.12, f32[896,1792]{1,0:T(8,128)} %param.7, f32[896,1792]{1,0:T(8,128)} %param.8, ...), kind=kLoop, calls=%fused_computation.1 | loop fusion | flops 28897792 | bytes 51398144 | tf_op jit(solution)/shard_map/reduce_max | solution.py:21
  27.9 17.5 %all-reduce = (f32[1792]{0:T(1024)S(1)}, f32[1792]{0:T(1024)S(1)}) all-reduce(f32[1792]{0:T(1024)S(1)} %get-tuple-element.10, f32[1792]{0:T(1024)S(1)} %get-tuple-element.6), channel_id=1, replica_groups=mesh['rows'=4,'tp'=8] {'rows'}, use_global_device_ids=true, to_apply=%region_1.0 | all-reduce | flops 3584 | bytes 28672 | tf_op jit(solution)/shard_map/pmax | solution.py:20
  45.4 0.0 copy-start.1
  45.4 0.0 copy-start.2
  45.4 5.0 %divide_convert_fusion.1 = bf16[896,1792]{1,0:T(8,128)(2,1)} fusion(f32[896,1792]{1,0:T(8,128)} %get-tuple-element.11, f32[1792]{0:T(1024)S(1)} %get-tuple-element.18), kind=kLoop, calls=%fused_computation.3 | loop fusion | flops 3211264 | bytes 9640960 | tf_op jit(solution)/shard_map/convert_element_type | solution.py:25
  50.4 0.0 all-gather.3.cloned.1.call-update
  50.4 0.0 copy-done.1
  50.4 0.0 all-gather.5.cloned.1.call-start
  50.4 0.0 copy-done.2
  50.5 5.0 %divide_convert_fusion = bf16[896,1792]{1,0:T(8,128)(2,1)} fusion(f32[896,1792]{1,0:T(8,128)} %get-tuple-element.7, f32[1792]{0:T(1024)S(1)} %get-tuple-element.19), kind=kLoop, calls=%fused_computation | loop fusion | flops 3211264 | bytes 9640960 | tf_op jit(solution)/shard_map/convert_element_type | solution.py:26
  55.4 0.0 all-gather.5.cloned.1.call-update
  55.5 119.0 %all-gather.3.cloned.1.call-done = bf16[3584,1792]{1,0:T(8,128)(2,1)} async-done(((bf16[896,1792]{1,0:T(8,128)(2,1)}), bf16[3584,1792]{1,0:T(8,128)(2,1)}) %all-gather.3.cloned.1.call-update) | async-done | bytes 12845072 | tf_op jit(solution)/shard_map/all_gather | solution.py:29
  174.5 127.0 %all-gather.5.cloned.1.call-done = bf16[3584,1792]{1,0:T(8,128)(2,1)} async-done(((bf16[896,1792]{1,0:T(8,128)(2,1)}), bf16[3584,1792]{1,0:T(8,128)(2,1)}) %all-gather.5.cloned.1.call-update) | async-done | bytes 12845072 | tf_op jit(solution)/shard_map/all_gather | solution.py:30
  301.5 0.0 copy-start
  301.5 11.2 %copy.13 = bf16[3584,1792]{1,0:T(8,128)(2,1)} copy(bf16[3584,1792]{1,0:T(8,128)(2,1)} %all-gather.3.cloned.1.call-done) | data formatting | bytes 25690112
  312.7 2.0 copy-done
  314.6 4.9 %copy.14 = bf16[3584,1792]{1,0:T(8,128)(2,1)} copy(bf16[3584,1792]{1,0:T(8,128)(2,1)S(1)} %copy-done) | data formatting | bytes 25690112
Async XLA Ops:
  7.2 167.3 %all-gather.3.cloned.1.call-start = ((), (), s32[]{:S(2)}) async-start(), calls=%async_computation | async-start | bytes 16056320 | tf_op jit(solution)/shard_map/all_gather | solution.py:29
  45.4 5.0 %copy-start.1 = (f32[1792]{0:T(1024)}, f32[1792]{0:T(1024)S(1)}, u32[]{:S(2)}) copy-start(f32[1792]{0:T(1024)S(1)} %get-tuple-element.18) | copy-start | bytes 21508
  45.4 5.1 %copy-start.2 = (f32[1792]{0:T(1024)}, f32[1792]{0:T(1024)S(1)}, u32[]{:S(2)}) copy-start(f32[1792]{0:T(1024)S(1)} %get-tuple-element.19) | copy-start | bytes 21508
  50.4 251.1 %all-gather.5.cloned.1.call-start = ((), (), s32[]{:S(2)}) async-start(), calls=%async_computation.1 | async-start | bytes 16056320 | tf_op jit(solution)/shard_map/all_gather | solution.py:30
  301.5 13.2 %copy-start = (bf16[3584,1792]{1,0:T(8,128)(2,1)S(1)}, bf16[3584,1792]{1,0:T(8,128)(2,1)}, u32[]{:S(2)}) copy-start(bf16[3584,1792]{1,0:T(8,128)(2,1)} %all-gather.5.cloned.1.call-done) | copy-start | bytes 38535172
Sparse Core Ops, SparseCore 0:
  50.5 123.9 all-gather.2
  176.9 124.5 all-gather.4
where the time goes:
time: 327 us; the launch traced here: 326 us
  waiting for transfers between devices  246 us (75%)
  other arithmetic  30.6 us (9%)
  local copies, waits for them, and re-layouts  18 us (6%)
  blocking collectives  17.5 us (5%)
  between operations  14.1 us (4%)
    all_gather x1, waiting for transfers between devices, per_device(): lax.all_gather(narrow_up, 'rows', axis=0, tiled=True)  127 us
    all_gather x1, waiting for transfers between devices, per_device(): lax.all_gather(narrow_gate, 'rows', axis=0, tiled=True)  119 us
    reduce_max x1, other arithmetic, per_device(): jnp.max(jnp.abs(whole_gained_up), axis=0)  20.6 us
    unnamed x8, local copies, waits for them, and re-layouts  18 us
    pmax x1, blocking collectives, per_device(): lax.pmax((jnp.max(jnp.abs(whole_gained_gate), axis=0), jnp.max(jnp.abs(wh...  17.5 us
  transfers between devices with their start and end apart: 2, of which 2 were waited for; matrix products, arithmetic and copies ran while one was open for 2% of the time, Pallas kernels for 0%

commit v1 on v0

v1 whole, which is shorter than its diff:
```python
import functools
import math

import jax
import jax.numpy as jnp
from jax import lax
from jax.experimental import pallas as pl
from jax.experimental.pallas import tpu as pltpu
from jax.sharding import PartitionSpec as P

learn_rate = 0.015
decay_rate = 0.1
tiny_value = 1e-08
MESH = pl.DeviceIdType.MESH
LANES = 128


def grid_of(rows):
    across = max(d for d in range(1, math.isqrt(rows) + 1) if rows % d == 0)
    return rows // across, across


def block_of(total, options):
    return next(b for b in options if total % b == 0)


def kernel(rows, width, step_rows, *refs):
    ins, gain, outs, columns = refs[:6], refs[6], refs[7:9], refs[9:11]
    stage, whole, peaks = refs[11:14]
    in_sem, peak_send, peak_recv, first_send, first_recv, next_send, next_recv = refs[14:]
    tall, wide = grid_of(rows)
    share, total = ins[0].shape
    chunks = total // width
    me = lax.axis_index("rows")
    my_y, my_x = me // wide, lax.rem(me, wide)

    def along_x(k):
        return my_y * wide + lax.rem(my_x + k, wide)

    def along_y(k):
        return lax.rem(my_y + k, tall) * wide + my_x

    plans = ((along_x, wide, along_y, tall), (along_y, tall, along_x, wide))

    def cols(c):
        return pl.ds(pl.multiple_of(c * width, LANES), width)

    def part(m, owner, c):
        return outs[m].at[pl.ds(pl.multiple_of(owner * share, step_rows), share), cols(c)]

    def load(c, slot):
        return [
            pltpu.make_async_copy(ins[a].at[:, cols(c)], stage.at[slot, a], in_sem.at[slot, a])
            for a in range(6)
        ]

    def send(ref, peer, send_sem, recv_sem):
        return pltpu.make_async_remote_copy(
            src_ref=ref, dst_ref=ref, send_sem=send_sem, recv_sem=recv_sem,
            device_id={"rows": peer}, device_id_type=MESH,
        )

    def peak_copy(c, k):
        return send(peaks.at[c, me], lax.rem(me + k, rows), peak_send.at[c, k], peak_recv.at[c, k])

    def peak_arrival(c, k):
        source = lax.rem(me + rows - k, rows)
        return send(peaks.at[c, source], source, peak_send.at[c, k], peak_recv.at[c, k])

    def first_copy(m, c, k, owner):
        return send(part(m, owner, c), plans[m][0](k), first_send.at[c, m, k], first_recv.at[c, m, k])

    def next_copy(m, c, j, k, owner):
        return send(part(m, owner, c), plans[m][2](k), next_send.at[c, m, j, k], next_recv.at[c, m, j, k])

    def owner_first(m, j):
        near, size = plans[m][:2]
        return near(size - j) if j else me

    def owner_next(m, j, k):
        y, x = my_y, my_x
        if m == 0:
            y, x = lax.rem(y + tall - k, tall), lax.rem(x + wide - j, wide)
        else:
            y, x = lax.rem(y + tall - j, tall), lax.rem(x + wide - k, wide)
        return y * wide + x

    for copy in load(0, 0):
        copy.start()

    @pl.when(chunks > 1)
    def _():
        for copy in load(min(1, chunks - 1), 1):
            copy.start()

    barrier = pltpu.get_barrier_semaphore()
    for k in range(1, rows):
        pl.semaphore_signal(
            barrier, inc=1, device_id={"rows": lax.rem(me + k, rows)}, device_id_type=MESH
        )
    pl.semaphore_wait(barrier, rows - 1)

    def update(c):
        slot = lax.rem(c, 2)
        for copy in load(c, slot):
            copy.wait()

        def step(i, most):
            at = pl.ds(pl.multiple_of(i * step_rows, step_rows), step_rows)
            g = gain[at, :]
            found = []
            for m in range(2):
                for t in range(width // LANES):
                    lane = pl.ds(t * LANES, LANES)
                    train, drift, spread = (stage[slot, 3 * m + a, at, lane] for a in range(3))
                    new = train - learn_rate * (
                        drift / (jnp.sqrt(spread) + tiny_value) + decay_rate * train
                    )
                    new = new * g
                    whole[slot, m, at, lane] = new
                    tops = jnp.max(jnp.abs(new).reshape(step_rows // 8, 8, LANES), axis=0)
                    found.append(jnp.maximum(most[len(found)], tops))
            return tuple(found)

        zero = jnp.zeros((8, LANES), jnp.float32)
        most = lax.fori_loop(0, share // step_rows, step, (zero,) * (2 * (width // LANES)))
        for m in range(2):
            for t in range(width // LANES):
                peaks[c, me, m : m + 1, pl.ds(t * LANES, LANES)] = jnp.max(
                    most[m * (width // LANES) + t], axis=0, keepdims=True
                )
        for k in range(1, rows):
            peak_copy(c, k).start()

    def finish(c):
        slot = lax.rem(c, 2)
        for k in range(1, rows):
            peak_arrival(c, k).wait_recv()
        scale = peaks[c, 0]
        for r in range(1, rows):
            scale = jnp.maximum(scale, peaks[c, r])
        for m in range(2):
            columns[m][:, cols(c)] = scale[m : m + 1, :]
        inverse = 1.0 / scale
        for m in range(2):
            factor = inverse[m : m + 1, :]

            def step(i, carry, m=m, factor=factor):
                at = pl.ds(pl.multiple_of(i * step_rows, step_rows), step_rows)
                to = pl.ds(pl.multiple_of(me * share + i * step_rows, step_rows), step_rows)
                outs[m][to, cols(c)] = (whole[slot, m, at, :] * factor).astype(jnp.bfloat16)
                return carry

            lax.fori_loop(0, share // step_rows, step, 0)
            for k in range(1, plans[m][1]):
                first_copy(m, c, k, me).start()

    update(0)

    def body(c, carry):
        @pl.when(c + 1 < chunks)
        def _():
            for copy in load(c + 1, lax.rem(c + 1, 2)):
                copy.start()

        update(c)
        finish(c - 1)
        return carry

    lax.fori_loop(1, chunks, body, 0)
    finish(chunks - 1)

    def own(c, carry):
        for m in range(2):
            for k in range(1, plans[m][3]):
                next_copy(m, c, 0, k, me).start()
        return carry

    lax.fori_loop(0, chunks, own, 0)

    def relay(c, carry):
        for j in range(1, max(tall, wide)):
            for m in range(2):
                if j < plans[m][1]:
                    first_copy(m, c, j, owner_first(m, j)).wait_recv()
                    for k in range(1, plans[m][3]):
                        next_copy(m, c, j, k, owner_first(m, j)).start()
        return carry

    lax.fori_loop(0, chunks, relay, 0)

    def drain(c, carry):
        for k in range(1, rows):
            peak_copy(c, k).wait_send()
        for m in range(2):
            for k in range(1, plans[m][1]):
                first_copy(m, c, k, me).wait_send()
            for j in range(plans[m][1]):
                for k in range(1, plans[m][3]):
                    next_copy(m, c, j, k, owner_first(m, j)).wait_send()
                    next_copy(m, c, j, k, owner_next(m, j, k)).wait_recv()
        return carry

    lax.fori_loop(0, chunks, drain, 0)


def settle(*arrays):
    pieces = 4

    def body(*refs):
        count = len(arrays)
        sem = refs[-1]
        copies = []
        for a in range(count):
            tall = arrays[a].shape[0] // pieces
            for p in range(pieces):
                at = pl.ds(p * tall, tall)
                copies.append(
                    pltpu.make_async_copy(refs[a].at[at], refs[count + a].at[at], sem.at[a, p])
                )
        for copy in copies:
            copy.start()
        for copy in copies:
            copy.wait()

    return pl.pallas_call(
        body,
        out_shape=tuple(jax.ShapeDtypeStruct(a.shape, a.dtype) for a in arrays),
        in_specs=[pl.BlockSpec(memory_space=pl.ANY)] * len(arrays),
        out_specs=(pl.BlockSpec(memory_space=pltpu.HBM),) * len(arrays),
        scratch_shapes=[pltpu.SemaphoreType.DMA((len(arrays), pieces))],
        compiler_params=pltpu.CompilerParams(vmem_limit_bytes=SMALL),
    )(*arrays)


def solution(mesh):
    rows = mesh.shape["rows"]

    def per_device(*args):
        arrays, norm_gain = args[:6], args[6]
        share, total = arrays[0].shape
        width = block_of(total, (256, LANES))
        step_rows = block_of(share, (32, 16))
        chunks = total // width
        most = max(grid_of(rows))
        gain = jnp.broadcast_to(norm_gain[:, None], (share, LANES))
        served = pltpu.VMEM((rows * share, total), jnp.bfloat16)
        column = pltpu.VMEM((1, total), jnp.float32)
        dma = pltpu.SemaphoreType.DMA
        serving_gate, serving_up, column_gate, column_up = pl.pallas_call(
            functools.partial(kernel, rows, width, step_rows),
            out_shape=OUT_SHAPES(served, column),
            in_specs=[pl.BlockSpec(memory_space=pltpu.HBM)] * 6
            + [pl.BlockSpec(memory_space=pltpu.VMEM)],
            out_specs=(pl.BlockSpec(memory_space=pltpu.VMEM),) * 4,
            scratch_shapes=[
                pltpu.VMEM((2, 6, share, width), jnp.float32),
                pltpu.VMEM((2, 2, share, width), jnp.float32),
                pltpu.VMEM((chunks, rows, 2, width), jnp.float32),
                dma((2, 6)),
                dma((chunks, rows)),
                dma((chunks, rows)),
                dma((chunks, 2, most)),
                dma((chunks, 2, most)),
                dma((chunks, 2, most, most)),
                dma((chunks, 2, most, most)),
            ],
            compiler_params=pltpu.CompilerParams(
                collective_id=0, has_side_effects=True, vmem_limit_bytes=VMEM_LIMIT
            ),
        )(*arrays, gain)
        serving_gate, serving_up = settle(serving_gate, serving_up)
        return serving_gate, serving_up, column_gate.reshape(total), column_up.reshape(total)

    split = P("rows", "tp")
    return jax.shard_map(
        per_device,
        mesh=mesh,
        in_specs=(split,) * 6 + (P("rows"),),
        out_specs=(P(None, "tp"), P(None, "tp"), P("tp"), P("tp")),
        check_vma=False,
    )


VMEM_LIMIT = 34 * 1024 * 1024
SMALL = 1024 * 1024


def OUT_SHAPES(served, column):
    return (served, served) + tuple(jax.ShapeDtypeStruct(r.shape, r.dtype) for r in (column, column))
```

time: 327 us -> 234 us (0.72)
  waiting for transfers between devices: 246 us -> 0 us
  Pallas kernels: 0 us -> 230 us
  other arithmetic: 30.6 us -> 1.24 us
  blocking collectives: 17.5 us -> 0 us
  local copies, waits for them, and re-layouts: 18 us -> 1.65 us
  between operations: 14.1 us -> 0.67 us
    all_gather x2 -> x0, waiting for transfers between devices: 246 us -> none  [the longest x1 127 us: per_device(): lax.all_gather(narrow_up, 'rows', axis=0, tiled=True)]
    pallas_call x0 -> x2, Pallas kernels: none -> 230 us  [the longest x1 221 us: per_device(): pl.pallas_call(functools.partial(kernel, rows, width, step_rows), out_sha...]
    reduce_max x1 -> x0, other arithmetic: 20.6 us -> none  [per_device(): jnp.max(jnp.abs(whole_gained_up), axis=0)]
    unnamed x8 -> x4, local copies, waits for them, and re-layouts: 18 us -> 0.01 us
    pmax x1 -> x0, blocking collectives: 17.5 us -> none  [per_device(): lax.pmax((jnp.max(jnp.abs(whole_gained_gate), axis=0), jnp.max(jnp.abs(wh...]
    convert_element_type x2 -> x0, other arithmetic: 9.97 us -> none  [the longest x1 4.99 us: per_device(): (whole_gained_up / column_up).astype(jnp.bfloat16)]
  transfers between devices with their start and end apart: 2 -> 0, of which waited for: 2 -> 0; matrix products, arithmetic and copies ran while one was open for 2% -> 0% of each run, Pallas kernels for 0% -> 0%
where the time goes in v1:
time: 234 us; the launch traced here: 233 us
  Pallas kernels  230 us (98%)
    pallas_call x1, Pallas kernels, per_device(): pl.pallas_call(functools.partial(kernel, rows, width, step_rows), out_sha...  221 us
    pallas_call x1, Pallas kernels, settle(): pl.pallas_call(body, out_shape=tuple((jax.ShapeDtypeStruct(a.shape, a.dty...  8.7 us

profile of v1, /device:TPU:0, one launch (start us, length us, event | category | flops | bytes accessed | tf_op | source)
XLA Modules:
  0.0 233.4 jit_solution(2383958918683081074)
XLA Ops:
  0.6 1.6 broadcast_in_dim.2.refs_6_
  2.3 221.2 %shard_map.102 = (bf16[3584,1792]{1,0:T(8,128)(2,1)S(1)}, bf16[3584,1792]{1,0:T(8,128)(2,1)S(1)}, f32[1,1792]{1,0:T(1,128)}, f32[1,1792]{1,0:T(1,128)}) custom-call(f32[896,1792]{1,0:T(8,128)} %refs_0_.1, f32[896,1792]{1,0:T(8,128)} %refs_1_.1, f32[896,1792]{1,0:T(8,128)} %refs_2_.1, f32[896,1792]{1,0:T(8,128)} %refs_3_.1, f32[896,1792]{1,0:T(8,128)} %refs_4_.1, ...), custom_call_target="tpu_custom_call" | custom-call | tf_op jit(solution)/shard_map/pallas_call | solution.py:250
  223.5 0.0 copy-start.1
  223.5 0.0 copy-start
  223.5 8.7 %shard_map.103 = (bf16[3584,1792]{1,0:T(8,128)(2,1)}, bf16[3584,1792]{1,0:T(8,128)(2,1)}) custom-call(bf16[3584,1792]{1,0:T(8,128)(2,1)S(1)} %get-tuple-element.10.refs_0_, bf16[3584,1792]{1,0:T(8,128)(2,1)S(1)} %get-tuple-element.11.refs_1_), custom_call_target="tpu_custom_call" | custom-call | tf_op jit(solution)/shard_map/pallas_call | solution.py:226
  232.2 0.0 copy-done.1
  232.2 0.6 reduce
  232.8 0.0 copy-done
  232.8 0.6 reduce.1
Async XLA Ops:
  223.5 8.7 %copy-start.1 = (f32[1,1792]{1,0:T(1,128)S(1)}, f32[1,1792]{1,0:T(1,128)}, u32[]{:S(2)}) copy-start(f32[1,1792]{1,0:T(1,128)} %get-tuple-element.14) | copy-start | bytes 21508
  223.5 9.4 %copy-start = (f32[1,1792]{1,0:T(1,128)S(1)}, f32[1,1792]{1,0:T(1,128)}, u32[]{:S(2)}) copy-start(f32[1,1792]{1,0:T(1,128)} %get-tuple-element.15) | copy-start | bytes 21508

commit v2 on v1

--- a/solution.py
+++ b/solution.py
@@ -25,9 +25,9 @@
 
 
 def kernel(rows, width, step_rows, *refs):
-    ins, gain, outs, columns = refs[:6], refs[6], refs[7:9], refs[9:11]
-    stage, whole, peaks = refs[11:14]
-    in_sem, peak_send, peak_recv, first_send, first_recv, next_send, next_recv = refs[14:]
+    ins, gains, outs, columns = refs[:6], refs[6], refs[7:9], refs[9:11]
+    stage, whole, peaks, gain = refs[11:15]
+    in_sem, peak_send, peak_recv, first_send, first_recv, next_send, next_recv = refs[15:]
     tall, wide = grid_of(rows)
     share, total = ins[0].shape
     chunks = total // width
@@ -99,6 +99,11 @@
             barrier, inc=1, device_id={"rows": lax.rem(me + k, rows)}, device_id_type=MESH
         )
     pl.semaphore_wait(barrier, rows - 1)
+
+    for start in range(0, share, LANES):
+        count = min(LANES, share - start)
+        line = gains[pl.ds(start, count)].reshape(1, count)
+        gain[pl.ds(start, count), :] = jnp.broadcast_to(line, (LANES, count)).T
 
     def update(c):
         slot = lax.rem(c, 2)
@@ -140,7 +145,7 @@
         for r in range(1, rows):
             scale = jnp.maximum(scale, peaks[c, r])
         for m in range(2):
-            columns[m][:, cols(c)] = scale[m : m + 1, :]
+            columns[m][cols(c)] = scale[m]
         inverse = 1.0 / scale
         for m in range(2):
             factor = inverse[m : m + 1, :]
@@ -204,16 +209,15 @@
     lax.fori_loop(0, chunks, drain, 0)
 
 
-def settle(*arrays):
-    pieces = 4
-
+def settle(pieces, *arrays):
     def body(*refs):
         count = len(arrays)
         sem = refs[-1]
         copies = []
         for a in range(count):
-            tall = arrays[a].shape[0] // pieces
-            for p in range(pieces):
+            parts = pieces if arrays[a].ndim > 1 else 1
+            tall = arrays[a].shape[0] // parts
+            for p in range(parts):
                 at = pl.ds(p * tall, tall)
                 copies.append(
                     pltpu.make_async_copy(refs[a].at[at], refs[count + a].at[at], sem.at[a, p])
@@ -239,17 +243,16 @@
     def per_device(*args):
         arrays, norm_gain = args[:6], args[6]
         share, total = arrays[0].shape
-        width = block_of(total, (256, LANES))
+        width = block_of(total, (LANES,))
         step_rows = block_of(share, (32, 16))
         chunks = total // width
         most = max(grid_of(rows))
-        gain = jnp.broadcast_to(norm_gain[:, None], (share, LANES))
         served = pltpu.VMEM((rows * share, total), jnp.bfloat16)
-        column = pltpu.VMEM((1, total), jnp.float32)
+        column = pltpu.VMEM((total,), jnp.float32)
         dma = pltpu.SemaphoreType.DMA
         serving_gate, serving_up, column_gate, column_up = pl.pallas_call(
             functools.partial(kernel, rows, width, step_rows),
-            out_shape=OUT_SHAPES(served, column),
+            out_shape=(served, served, column, column),
             in_specs=[pl.BlockSpec(memory_space=pltpu.HBM)] * 6
             + [pl.BlockSpec(memory_space=pltpu.VMEM)],
             out_specs=(pl.BlockSpec(memory_space=pltpu.VMEM),) * 4,
@@ -257,6 +260,7 @@
                 pltpu.VMEM((2, 6, share, width), jnp.float32),
                 pltpu.VMEM((2, 2, share, width), jnp.float32),
                 pltpu.VMEM((chunks, rows, 2, width), jnp.float32),
+                pltpu.VMEM((share, LANES), jnp.float32),
                 dma((2, 6)),
                 dma((chunks, rows)),
                 dma((chunks, rows)),
@@ -268,9 +272,8 @@
             compiler_params=pltpu.CompilerParams(
                 collective_id=0, has_side_effects=True, vmem_limit_bytes=VMEM_LIMIT
             ),
-        )(*arrays, gain)
-        serving_gate, serving_up = settle(serving_gate, serving_up)
-        return serving_gate, serving_up, column_gate.reshape(total), column_up.reshape(total)
+        )(*arrays, norm_gain)
+        return settle(2 * rows, serving_gate, serving_up, column_gate, column_up)
 
     split = P("rows", "tp")
     return jax.shard_map(
@@ -284,7 +287,3 @@
 
 VMEM_LIMIT = 34 * 1024 * 1024
 SMALL = 1024 * 1024
-
-
-def OUT_SHAPES(served, column):
-    return (served, served) + tuple(jax.ShapeDtypeStruct(r.shape, r.dtype) for r in (column, column))

time: 234 us -> 230 us (0.983)
  no operation moved by 1% of the time
where the time goes in v2:
time: 230 us
  Pallas kernels  230 us (100%)
    pallas_call x1, Pallas kernels, per_device(): pl.pallas_call(functools.partial(kernel, rows, width, step_rows), out_sha...  221 us
    pallas_call x1, Pallas kernels, settle(): pl.pallas_call(body, out_shape=tuple((jax.ShapeDtypeStruct(a.shape, a.dty...  8.82 us

profile of v2, /device:TPU:0, one launch (start us, length us, event | category | flops | bytes accessed | tf_op | source)
XLA Modules:
  0.0 230.1 jit_solution(14369700719078584031)
XLA Ops:
  0.6 220.7 %shard_map.102 = (bf16[3584,1792]{1,0:T(8,128)(2,1)S(1)}, bf16[3584,1792]{1,0:T(8,128)(2,1)S(1)}, f32[1792]{0:T(1024)S(1)}, f32[1792]{0:T(1024)S(1)}) custom-call(f32[896,1792]{1,0:T(8,128)} %refs_0_.1, f32[896,1792]{1,0:T(8,128)} %refs_1_.1, f32[896,1792]{1,0:T(8,128)} %refs_2_.1, f32[896,1792]{1,0:T(8,128)} %refs_3_.1, f32[896,1792]{1,0:T(8,128)} %refs_4_.1, ...), custom_call_target="tpu_custom_call" | custom-call | tf_op jit(solution)/shard_map/pallas_call | solution.py:253
  221.3 8.8 %shard_map.103 = (bf16[3584,1792]{1,0:T(8,128)(2,1)}, bf16[3584,1792]{1,0:T(8,128)(2,1)}, f32[1792]{0:T(1024)}, f32[1792]{0:T(1024)}) custom-call(bf16[3584,1792]{1,0:T(8,128)(2,1)S(1)} %get-tuple-element.8.refs_0_, bf16[3584,1792]{1,0:T(8,128)(2,1)S(1)} %get-tuple-element.9.refs_1_, f32[1792]{0:T(1024)S(1)} %get-tuple-element.10.refs_2_, ...), custom_call_target="tpu_custom_call" | custom-call | tf_op jit(solution)/shard_map/pallas_call | solution.py:230
